TPU v7x, 128 devices: a whole 4x4x4 slice. The times are simulated.
128 devices in a mesh: px: 16 (over z, y), py: 8 (over x, core).
Axes of the slice: x: 4, y: 4, z: 4, core: 2. Of those that a mesh axis runs over, the one named last changes fastest.
Arguments:
- point_channel_values: bfloat16 [16384, 64, 128], P(('px', 'py')), may hold values from -6 to 6
- point_offsets: bfloat16 [16384, 3, 128], P(('px', 'py')), may hold values from -1 to 17
- point_counts: int32 [16384], P(('px', 'py')), may hold values from 1 to 128
- block_bricks: int32 [16384, 4], P(('px', 'py')), may hold values from 0 to 16383, as said below
- spectral_weights: bfloat16 [2, 32, 32, 32, 64, 128], P(None, None, 'px', 'py'), may hold values from -0.5 to 0.5
- skip_weights: bfloat16 [2, 64, 64], replicated, may hold values from -0.75 to 0.75
- skip_bias: float32 [2, 64], replicated, may hold values from -3 to 3
Outputs:
- decoded: bfloat16 [16384, 64, 128], P(('px', 'py'))
Inputs may be any that keep to these rules, and one draw needn't show every extreme that they name: `block_bricks`: the 4 bricks of a block are distinct and lie on one device. Among the 128 blocks of one device at most 2 have their bricks on any one device, and in every draw some device receives exactly 2 blocks from every device.
All inputs are finite; a program needn't handle non-finite values.
Results may differ from a plain program's by a relative error of at most 0.0075.
Values may be sent and summed in bfloat16 or wider, within the bound.
No kernel may reach another device: no remote copies, remote signals or barrier semaphores. Data moves between devices by JAX's collectives and lax.ppermute only.
A program may use at most 256 MiB of HBM per device.

v0:
```python
import math

import jax
import jax.numpy as jnp
from jax import lax
from jax.sharding import PartitionSpec as P

MODES = 32
NX = 128
NY = 128
NZ = 128
LAYERS = 2


AMPLITUDE = 0.25
SPREAD = 4.5
DECODE_SCALE = 0.1
PRECISE = lax.Precision.HIGHEST


def in_one_piece(arrays, axis, split_dim, concat_dim, along):
    ends, at = ([], 0)
    for a in arrays[:-1]:
        at += a.shape[along]
        ends.append(at)
    both = jnp.concatenate(arrays, axis=along)
    return tuple(
        jnp.split(
            lax.all_to_all(both, axis, split_axis=split_dim, concat_axis=concat_dim, tiled=True),
            ends,
            axis=along,
        )
    )


def in_one_piece_2(arrays, axis, split_dim, concat_dim, along):
    widths = [math.prod(a.shape[along:]) for a in arrays]
    both = jnp.concatenate(
        [a.reshape(*a.shape[:along], w) for a, w in zip(arrays, widths)], axis=along
    )
    result = lax.all_to_all(both, axis, split_axis=split_dim, concat_axis=concat_dim, tiled=True)
    tiles = jnp.split(result, [sum(widths[:k]) for k in range(1, len(widths))], axis=along)
    return tuple(
        (b.reshape(*result.shape[:along], *a.shape[along:]) for a, b in zip(arrays, tiles))
    )


def wave_numbers(kept_modes):
    position = jnp.arange(kept_modes, dtype=jnp.int32)
    return jnp.where(position < kept_modes // 2, position, position - kept_modes)


def forward_matrix(length, frequency):
    places = jnp.arange(length, dtype=jnp.int32)
    products = jnp.remainder(places[:, None] * frequency[None, :], length)
    angles = 2.0 * math.pi / length * products.astype(jnp.float32)
    cosine = jnp.cos(angles) / math.sqrt(length)
    sine_part = jnp.sin(angles) / math.sqrt(length)
    from_real = jnp.stack([cosine, -sine_part], axis=-1)
    from_imag = jnp.stack([sine_part, cosine], axis=-1)
    return jnp.stack([from_real, from_imag], axis=1)


def cell_centers():
    cell_index = jnp.arange(128, dtype=jnp.int32)
    return (
        jnp.stack([cell_index // 64, cell_index // 16 % 4, cell_index % 16]).astype(jnp.float32)
        + 0.5
    )


def brick_anchor(local_ids, bricks_y, bricks_z):
    clamped_weights = jnp.maximum(local_ids, 0)
    return jnp.stack(
        [
            2 * (clamped_weights // (bricks_y * bricks_z)),
            4 * (clamped_weights // bricks_z % bricks_y),
            16 * (clamped_weights % bricks_z),
        ],
        axis=-1,
    ).astype(jnp.float32)


def block_work(features, offsets, counts, local_ids, bricks_y, bricks_z):
    total_items, channels, points = features.shape
    group_size = math.gcd(total_items, 16)
    centers = cell_centers()

    def one_group(items):
        feature_share, offset_part, count_part, id_part = items
        validity = (jnp.arange(points, dtype=jnp.int32)[None, :] < count_part[:, None]).astype(
            jnp.float32
        )
        anchors = brick_anchor(id_part, bricks_y, bricks_z)
        relative_position = anchors - anchors[:, :1, :]
        placed = offset_part.astype(jnp.float32)[:, None, :, :] - relative_position[:, :, :, None]
        apart = placed[..., None] - centers[None, None, :, None, :]
        distance = jnp.sum(apart * apart, axis=2)
        kernel_weight_value = (
            AMPLITUDE * jnp.exp(-distance / SPREAD) * validity[:, None, :, None]
        ).astype(jnp.bfloat16)
        brick_tile_grid = jnp.einsum(
            "dqw,dewn->deqn", feature_share, kernel_weight_value, preferred_element_type=jnp.float32
        ).astype(jnp.bfloat16)
        return (kernel_weight_value, brick_tile_grid)

    grouped = tuple(
        (
            member.reshape((total_items // group_size, group_size) + member.shape[1:])
            for member in (features, offsets, counts, local_ids)
        )
    )
    kernel_weight_value, brick_tile_grid = lax.map(one_group, grouped)
    return (
        kernel_weight_value.reshape((total_items,) + kernel_weight_value.shape[2:]),
        brick_tile_grid.reshape((total_items,) + brick_tile_grid.shape[2:]),
    )


def decode_points(brick_values, kernel_weight_value):
    summed = jnp.einsum(
        "nhcx,nhpx->ncp", brick_values, kernel_weight_value, preferred_element_type=jnp.float32
    )
    return (DECODE_SCALE * summed).astype(jnp.bfloat16)


def accumulate(brick_tile_grid, local_ids, bricks_device):
    flat_ids = local_ids.reshape(-1)
    selector = (flat_ids[:, None] == jnp.arange(bricks_device, dtype=jnp.int32)[None, :]).astype(
        jnp.bfloat16
    )
    flat_tiles = brick_tile_grid.reshape((flat_ids.shape[0],) + brick_tile_grid.shape[2:])
    return jnp.einsum("rb,rcx->bcx", selector, flat_tiles, preferred_element_type=jnp.float32)


def to_grid(bricks, bricks_along_first, bricks_y, bricks_z):
    channels = bricks.shape[1]
    shaped = bricks.reshape(bricks_along_first, bricks_y, bricks_z, channels, 2, 4, 16)
    return shaped.transpose(3, 0, 4, 1, 5, 2, 6).reshape(
        channels, 2 * bricks_along_first, 4 * bricks_y, 16 * bricks_z
    )


def to_bricks(grid, bricks_along_first, bricks_y, bricks_z):
    channels = grid.shape[0]
    shaped = grid.reshape(channels, bricks_along_first, 2, bricks_y, 4, bricks_z, 16)
    return shaped.transpose(1, 3, 5, 0, 2, 4, 6).reshape(
        bricks_along_first * bricks_y * bricks_z, channels, 128
    )


def spectral(grid, weights, tables):
    table_third, forward_second, forward_first, back_second, back_first, back_third = tables
    channels, cells_x = (grid.shape[0], grid.shape[1])
    third_modes = jnp.einsum(
        "cxyz,zq->cxyq", grid.astype(jnp.float32), table_third, precision=PRECISE
    ).astype(jnp.bfloat16)
    columns = lax.all_to_all(third_modes, "py", split_axis=3, concat_axis=2, tiled=True)
    third_local = columns.shape[3] // 2
    second_modes = jnp.einsum(
        "cxyzp,ypkq->cxzkq",
        columns.reshape(channels, cells_x, columns.shape[2], third_local, 2).astype(jnp.float32),
        forward_second,
        precision=PRECISE,
    ).astype(jnp.bfloat16)
    row_lines = lax.all_to_all(second_modes, "px", split_axis=3, concat_axis=1, tiled=True)
    first_modes = jnp.einsum(
        "cxzkp,xpmq->mkzcq", row_lines.astype(jnp.float32), forward_first, precision=PRECISE
    ).astype(jnp.bfloat16)
    product = jnp.einsum(
        "mkzcp,mkzcr->mkzpr", first_modes, weights, preferred_element_type=jnp.float32
    )
    product = product.reshape(product.shape[:4] + (2, channels))
    mixed_real = product[:, :, :, 0, 0] - product[:, :, :, 1, 1]
    mixed_imag = product[:, :, :, 0, 1] + product[:, :, :, 1, 0]
    mixed = jnp.stack([mixed_real, mixed_imag], axis=-1)
    first_back = jnp.einsum("mkzcp,mpxq->cxzkq", mixed, back_first, precision=PRECISE).astype(
        jnp.bfloat16
    )
    row_back = lax.all_to_all(first_back, "px", split_axis=1, concat_axis=3, tiled=True)
    second_back = jnp.einsum(
        "cxzkp,kpyq->cxyzq", row_back.astype(jnp.float32), back_second, precision=PRECISE
    )
    second_back = second_back.reshape(channels, cells_x, second_back.shape[2], -1).astype(
        jnp.bfloat16
    )
    column_back = lax.all_to_all(second_back, "py", split_axis=2, concat_axis=3, tiled=True)
    return jnp.einsum(
        "cxyq,qz->cxyz", column_back.astype(jnp.float32), back_third, precision=PRECISE
    )


def slot_plan(block_bricks, bricks_device, slot_total, capacity):
    owners = block_bricks[:, 0] // bricks_device
    order_index = jnp.arange(owners.shape[0], dtype=jnp.int32)
    earlier = (owners[None, :] == owners[:, None]) & (order_index[None, :] < order_index[:, None])
    ranking = jnp.sum(earlier.astype(jnp.int32), axis=1)
    slot_index = owners * capacity + ranking
    matching = slot_index[None, :] == jnp.arange(slot_total, dtype=jnp.int32)[:, None]
    present = jnp.any(matching, axis=1)
    sources = jnp.sum(jnp.where(matching, order_index[None, :], 0), axis=1)
    return (slot_index, present, sources)


def pack_slots(values, present, sources, filler):
    picked = jnp.take(values, sources, axis=0)
    masking = present.reshape((-1,) + (1,) * (values.ndim - 1))
    return jnp.where(masking, picked, jnp.asarray(filler, values.dtype))


def route_back(values):
    return lax.all_to_all(values, ("px", "py"), split_axis=0, concat_axis=0, tiled=True)


def per_device(
    point_channel_values,
    point_offsets,
    point_counts,
    block_bricks,
    spectral_weights,
    skip_weights,
    skip_bias,
):
    mesh_rows = lax.axis_size("px")
    mesh_columns = lax.axis_size("py")
    device_total = mesh_rows * mesh_columns
    capacity = max(2, 2 * point_channel_values.shape[0] // device_total)
    bricks_along_first = NX // mesh_rows // 2
    bricks_y = NY // mesh_columns // 4
    bricks_z = NZ // 16
    bricks_device = bricks_along_first * bricks_y * bricks_z
    slot_total = device_total * capacity
    local_ids = block_bricks % bricks_device
    slot_index, present, sources = slot_plan(block_bricks, bricks_device, slot_total, capacity)
    packed_ids = pack_slots(local_ids, present, sources, -1)
    packed_features = pack_slots(point_channel_values, present, sources, 0)
    packed_offsets = pack_slots(point_offsets, present, sources, 0)
    packed_counts = pack_slots(point_counts, present, sources, 0)
    got_features, got_offsets, got_counts, got_ids = (
        *in_one_piece((packed_features, packed_offsets), ("px", "py"), 0, 0, 1),
        *in_one_piece_2((packed_counts, packed_ids), ("px", "py"), 0, 0, 1),
    )
    got_weight, got_tiles = block_work(
        got_features, got_offsets, got_counts, got_ids, bricks_y, bricks_z
    )
    encoded = accumulate(got_tiles, got_ids, bricks_device).astype(jnp.bfloat16)
    grid = to_grid(encoded, bricks_along_first, bricks_y, bricks_z)
    third_matrix = forward_matrix(NZ, jnp.arange(MODES, dtype=jnp.int32))[:, 0]
    weighting = jnp.where(jnp.arange(MODES) == 0, 1.0, 2.0).astype(jnp.float32)
    forward_second = forward_matrix(NY, wave_numbers(MODES))
    forward_first = forward_matrix(NX, wave_numbers(MODES))
    tables = (
        third_matrix.reshape(NZ, 2 * MODES),
        forward_second,
        forward_first,
        forward_second.transpose(2, 3, 0, 1),
        forward_first.transpose(2, 3, 0, 1),
        (third_matrix * weighting[None, :, None]).reshape(NZ, 2 * MODES).T,
    )
    for depth_index in range(LAYERS):
        spectral_part = spectral(grid, spectral_weights[depth_index], tables)
        skipped = jnp.einsum(
            "io,ixyz->oxyz", skip_weights[depth_index], grid, preferred_element_type=jnp.float32
        )
        grid = jax.nn.gelu(
            spectral_part + skipped + skip_bias[depth_index][:, None, None, None], approximate=False
        ).astype(jnp.bfloat16)
    final_bricks = to_bricks(grid, bricks_along_first, bricks_y, bricks_z)
    wanted = jnp.take(final_bricks, jnp.maximum(got_ids, 0), axis=0)
    reply = decode_points(wanted, got_weight)
    returned = route_back(reply)
    return jnp.take(returned, slot_index, axis=0)


def solution(mesh):
    return jax.shard_map(
        per_device,
        mesh=mesh,
        in_specs=(
            P(("px", "py"), None, None),
            P(("px", "py"), None, None),
            P(("px", "py")),
            P(("px", "py"), None),
            P(None, None, "px", "py", None, None),
            P(),
            P(),
        ),
        out_specs=P(("px", "py"), None, None),
        check_vma=False,
    )
```

profile of v0, /device:TPU:1, one launch (start us, length us, event | category | flops | bytes accessed | tf_op | source)
XLA Modules:
  0.0 693.7 jit_solution(181016568622383781)
XLA Ops:
  9.9 11.5 %all-to-all-start = ((s32[128,2,5]{2,1,0:T(2,128)}), s32[128,2,5]{2,1,0:T(2,128)S(1)}, u32[]{:S(2)}, u32[]{:S(2)}) async-start(s32[128,2,5]{2,1,0:T(2,128)} %pad_add_fusion), calls=%async_computation | async-start | bytes 262144 | tf_op jit(solution)/shard_map/all_to_all | solution.py:41
  32.6 10.2 %all-to-all-start.1 = ((bf16[256,67,128]{2,1,0:T(8,128)(2,1)}), bf16[256,67,128]{2,1,0:T(8,128)(2,1)}, u32[]{:S(2)}, u32[]{:S(2)}) async-start(bf16[256,67,128]{2,1,0:T(8,128)(2,1)} %pad_maximum_fusion), calls=%async_computation.1 | async-start | bytes 9437184 | tf_op jit(solution)/shard_map/all_to_all | solution.py:29
  44.2 56.8 %all-to-all-done.1 = bf16[256,67,128]{2,1,0:T(8,128)(2,1)} async-done(((bf16[256,67,128]{2,1,0:T(8,128)(2,1)}), bf16[256,67,128]{2,1,0:T(8,128)(2,1)}, u32[]{:S(2)}, u32[]{:S(2)}) %all-to-all-start.1) | async-done | bytes 4390944 | tf_op jit(solution)/shard_map/all_to_all | solution.py:29
  102.1 5.1 split.19
  107.2 155.0 %while.15 = (s32[]{:T(128)}, bf16[16,16,4,128,128]{4,3,2,1,0:T(8,128)(2,1)}, bf16[16,16,4,64,128]{4,3,2,1,0:T(8,128)(2,1)}, bf16[16,16,3,128]{3,2,1,0:T(4,128)(2...) while((s32[]{:T(128)}, ...), condition=%wide.region_5.6_spmd, body=%wide.region_3.5_spmd.sunk | while | flops 151557504 | bytes 16283637 | solution.py:113
  262.2 16.2 %fusion.60 = bf16[128,64,128]{2,0,1:T(8,128)(2,1)S(1)} fusion(bf16[1024,64,128]{2,1,0:T(8,128)(2,1)} %bitcast.406, s32[1024]{0:T(1024)S(1)} %eq.76), kind=kOutput, calls=%fused_computation.118 | convolution fusion | flops 2148663296 | bytes 18878464 | tf_op jit(solution)/shard_map/rb,rcx->bcx/dot_general | solution.py:133
  282.4 5.4 copy.483
  287.7 4.8 copy.485
  295.7 4.9 copy.486
  303.3 4.4 all-to-all-start.2
  307.9 14.8 %all-to-all-done.2 = bf16[8,2,32768]{2,1,0:T(2,128)(2,1)S(1)} async-done(((bf16[8,2,32768]{2,1,0:T(2,128)(2,1)}), bf16[8,2,32768]{2,1,0:T(2,128)(2,1)S(1)}, u32[]{:S(2)}, u32[]{:S(2)}) %all-to-all-start.2) | async-done | bytes 1048608 | tf_op jit(solution)/shard_map/all_to_all | solution.py:158
  331.9 10.1 %all_to_all.157 = bf16[16,2,4096]{2,1,0:T(2,128)(2,1)S(1)} all-to-all(bf16[16,2,4096]{2,1,0:T(2,128)(2,1)S(1)} %reshape.988), channel_id=1, replica_groups=mesh['px'=16,'py'=8] {'px'}, dimensions={0} | all-to-all | bytes 524288 | tf_op jit(solution)/shard_map/all_to_all | solution.py:166
  348.6 10.7 %all_to_all.158 = bf16[16,2,4096]{2,1,0:T(2,128)(2,1)S(1)} all-to-all(bf16[16,2,4096]{2,1,0:T(2,128)(2,1)S(1)} %reshape.990), channel_id=1, replica_groups=mesh['px'=16,'py'=8] {'px'}, dimensions={0} | all-to-all | bytes 524288 | tf_op jit(solution)/shard_map/all_to_all | solution.py:180
  368.2 7.1 %all-to-all-start.5 = ((bf16[8,2,32768]{2,1,0:T(2,128)(2,1)}), bf16[8,2,32768]{2,1,0:T(2,128)(2,1)S(1)}, u32[]{:S(2)}, u32[]{:S(2)}) async-start(bf16[8,2,32768]{2,1,0:T(2,128)(2,1)} %reshape.992), calls=%async_computation.5 | async-start | bytes 2097152 | tf_op jit(solution)/shard_map/all_to_all | solution.py:187
  376.2 5.8 fusion.110
  381.9 8.4 %all-to-all-done.5 = bf16[8,2,32768]{2,1,0:T(2,128)(2,1)S(1)} async-done(((bf16[8,2,32768]{2,1,0:T(2,128)(2,1)}), bf16[8,2,32768]{2,1,0:T(2,128)(2,1)S(1)}, u32[]{:S(2)}, u32[]{:S(2)}) %all-to-all-start.5) | async-done | bytes 1048608 | tf_op jit(solution)/shard_map/all_to_all | solution.py:187
  397.4 6.5 fusion.73
  403.9 9.2 %fusion.31 = bf16[64,8,16,128]{3,2,1,0:T(8,128)(2,1)S(1)} fusion(f32[64,8,16,128]{3,2,1,0:T(8,128)S(1)} %get-tuple-element.246, u8[64,16,128]{2,1,0:T(8,128)(4,1)S(1)} %get-tuple-element.245), kind=kLoop, calls=%fused_computation.63 | loop fusion | flops 71303168 | bytes 6422528 | tf_op jit(solution)/shard_map/convert_element_type | solution.py:267
  416.1 5.4 copy.513
  424.8 19.2 %all_to_all.159 = bf16[8,2,32768]{2,1,0:T(2,128)(2,1)} all-to-all(bf16[8,2,32768]{2,1,0:T(2,128)(2,1)S(1)} %reshape.994), channel_id=1, replica_groups=mesh['px'=16,'py'=8] {'py'}, dimensions={0} | all-to-all | bytes 2097152 | tf_op jit(solution)/shard_map/all_to_all | solution.py:158
  459.8 10.3 %all_to_all.160 = bf16[16,2,4096]{2,1,0:T(2,128)(2,1)S(1)} all-to-all(bf16[16,2,4096]{2,1,0:T(2,128)(2,1)S(1)} %reshape.996), channel_id=1, replica_groups=mesh['px'=16,'py'=8] {'px'}, dimensions={0} | all-to-all | bytes 524288 | tf_op jit(solution)/shard_map/all_to_all | solution.py:166
  476.6 10.3 %all_to_all.161 = bf16[16,2,4096]{2,1,0:T(2,128)(2,1)S(1)} all-to-all(bf16[16,2,4096]{2,1,0:T(2,128)(2,1)S(1)} %reshape.998), channel_id=1, replica_groups=mesh['px'=16,'py'=8] {'px'}, dimensions={0} | all-to-all | bytes 524288 | tf_op jit(solution)/shard_map/all_to_all | solution.py:180
  489.7 4.7 copy.532
  498.7 7.3 %all-to-all-start.9 = ((bf16[8,2,32768]{2,1,0:T(2,128)(2,1)}), bf16[8,2,32768]{2,1,0:T(2,128)(2,1)S(1)}, u32[]{:S(2)}, u32[]{:S(2)}) async-start(bf16[8,2,32768]{2,1,0:T(2,128)(2,1)} %reshape.1000), calls=%async_computation.9 | async-start | bytes 2097152 | tf_op jit(solution)/shard_map/all_to_all | solution.py:187
  510.0 11.0 %all-to-all-done.9 = bf16[8,2,32768]{2,1,0:T(2,128)(2,1)S(1)} async-done(((bf16[8,2,32768]{2,1,0:T(2,128)(2,1)}), bf16[8,2,32768]{2,1,0:T(2,128)(2,1)S(1)}, u32[]{:S(2)}, u32[]{:S(2)}) %all-to-all-start.9) | async-done | bytes 1048608 | tf_op jit(solution)/shard_map/all_to_all | solution.py:187
  528.8 13.4 %fusion.34 = bf16[64,8,16,128]{3,2,1,0:T(8,128)(2,1)S(1)} fusion(f32[8,16,128,64]{2,3,1,0:T(8,128)} %fusion.58, bf16[64,8,16,64]{3,2,1,0:T(8,128)(2,1)} %copy.535, f32[128,64,1,1]{0,1,3,2:T(8,128)S(1)} %bitcast.401, f32[64]{0:T(128)S(1)} %get-tuple-element.240), kind=kOutput, calls=%fused_computation.66 | convolution fusion | flops 875560960 | bytes 7373056 | tf_op jit(solution)/shard_map/cxyq,qz->cxyz/dot_general | solution.py:188
  546.2 5.4 copy.540
  551.6 22.9 %gather_fusion.4 = bf16[1024,64,128]{1,2,0:T(8,128)(2,1)} fusion(bf16[128,64,128]{1,2,0:T(8,128)(2,1)} %bitcast.358, s32[1024]{0:T(1024)S(1)} %broadcast_clamp_fusion), kind=kCustom, calls=%fused_computation.4 | custom fusion | bytes 33558528 | tf_op jit(solution)/shard_map/jit(_take)/gather | solution.py:269
  574.5 30.5 %copy.541 = bf16[256,4,64,128]{3,2,1,0:T(8,128)(2,1)} copy(bf16[256,4,64,128]{2,3,1,0:T(8,128)(2,1)} %bitcast.359) | data formatting | bytes 33554432 | tf_op jit(solution)/shard_map/jit(_take)/gather | solution.py:269
  605.0 22.3 %fusion.27 = bf16[256,64,128]{2,1,0:T(8,128)(2,1)} fusion(bf16[256,4,128,128]{3,2,1,0:T(8,128)(2,1)} %bitcast.405, bf16[256,4,64,128]{3,2,1,0:T(8,128)(2,1)} %copy.541, pred[256,4]{1,0:T(8,128)(4,1)S(1)} %broadcast_compare_fusion), kind=kOutput, calls=%fused_computation.56 | convolution fusion | flops 2160066560 | bytes 54526976 | tf_op jit(solution)/shard_map/nhcx,nhpx->ncp/dot_general | solution.py:121
  627.4 5.7 all-to-all-start.10
  633.8 52.0 %all-to-all-done.10 = bf16[256,64,128]{2,1,0:T(8,128)(2,1)} async-done(((bf16[256,64,128]{2,1,0:T(8,128)(2,1)}), bf16[256,64,128]{2,1,0:T(8,128)(2,1)}, u32[]{:S(2)}, u32[]{:S(2)}) %all-to-all-start.10) | async-done | bytes 4194336 | tf_op jit(solution)/shard_map/all_to_all | solution.py:212
  (339 shorter events, 278.9 us)
Async XLA Ops:
  0.0 23.1 %copy-start = (bf16[128,64,128]{2,1,0:T(8,128)(2,1)S(1)}, bf16[128,64,128]{2,1,0:T(8,128)(2,1)}, u32[]{:S(2)}) copy-start(bf16[128,64,128]{2,1,0:T(8,128)(2,1)} %param.9) | copy-start | bytes 6291460
  0.0 21.4 %copy-start.2 = (bf16[128,3,128]{2,0,1:T(8,128)(2,1)S(1)}, bf16[128,3,128]{2,0,1:T(8,128)(2,1)}, u32[]{:S(2)}) copy-start(bf16[128,3,128]{2,0,1:T(8,128)(2,1)} %param.10) | copy-start | bytes 294916
  1.7 0.9 copy-start.5
  9.9 22.7 %all-to-all-start = ((s32[128,2,5]{2,1,0:T(2,128)}), s32[128,2,5]{2,1,0:T(2,128)S(1)}, u32[]{:S(2)}, u32[]{:S(2)}) async-start(s32[128,2,5]{2,1,0:T(2,128)} %pad_add_fusion), calls=%async_computation | async-start | bytes 262144 | tf_op jit(solution)/shard_map/all_to_all | solution.py:41
  32.6 68.4 %all-to-all-start.1 = ((bf16[256,67,128]{2,1,0:T(8,128)(2,1)}), bf16[256,67,128]{2,1,0:T(8,128)(2,1)}, u32[]{:S(2)}, u32[]{:S(2)}) async-start(bf16[256,67,128]{2,1,0:T(8,128)(2,1)} %pad_maximum_fusion), calls=%async_computation.1 | async-start | bytes 9437184 | tf_op jit(solution)/shard_map/all_to_all | solution.py:29
  303.3 19.4 %all-to-all-start.2 = ((bf16[8,2,32768]{2,1,0:T(2,128)(2,1)}), bf16[8,2,32768]{2,1,0:T(2,128)(2,1)S(1)}, u32[]{:S(2)}, u32[]{:S(2)}) async-start(bf16[8,2,32768]{2,1,0:T(2,128)(2,1)} %reshape.986), calls=%async_computation.2 | async-start | bytes 2097152 | tf_op jit(solution)/shard_map/all_to_all | solution.py:158
  362.0 14.1 %copy-start.4 = (f32[2,64]{1,0:T(2,128)S(1)}, f32[2,64]{1,0:T(2,128)}, u32[]{:S(2)}) copy-start(f32[2,64]{1,0:T(2,128)} %param.15) | copy-start | bytes 1540
  368.2 22.1 %all-to-all-start.5 = ((bf16[8,2,32768]{2,1,0:T(2,128)(2,1)}), bf16[8,2,32768]{2,1,0:T(2,128)(2,1)S(1)}, u32[]{:S(2)}, u32[]{:S(2)}) async-start(bf16[8,2,32768]{2,1,0:T(2,128)(2,1)} %reshape.992), calls=%async_computation.5 | async-start | bytes 2097152 | tf_op jit(solution)/shard_map/all_to_all | solution.py:187
  489.7 16.6 %copy-start.3 = (bf16[2,64,64]{2,1,0:T(8,128)(2,1)S(1)}, bf16[2,64,64]{2,1,0:T(8,128)(2,1)}, u32[]{:S(2)}) copy-start(bf16[2,64,64]{2,1,0:T(8,128)(2,1)} %param.14) | copy-start | bytes 49156
  498.7 22.3 %all-to-all-start.9 = ((bf16[8,2,32768]{2,1,0:T(2,128)(2,1)}), bf16[8,2,32768]{2,1,0:T(2,128)(2,1)S(1)}, u32[]{:S(2)}, u32[]{:S(2)}) async-start(bf16[8,2,32768]{2,1,0:T(2,128)(2,1)} %reshape.1000), calls=%async_computation.9 | async-start | bytes 2097152 | tf_op jit(solution)/shard_map/all_to_all | solution.py:187
  627.4 5.7 copy-start.6
  627.4 58.4 %all-to-all-start.10 = ((bf16[256,64,128]{2,1,0:T(8,128)(2,1)}), bf16[256,64,128]{2,1,0:T(8,128)(2,1)}, u32[]{:S(2)}, u32[]{:S(2)}) async-start(bf16[256,64,128]{2,1,0:T(8,128)(2,1)} %fusion.27), calls=%async_computation.10 | async-start | bytes 8388608 | tf_op jit(solution)/shard_map/all_to_all | solution.py:212
  633.7 59.5 %copy-start.1 = (bf16[128,64,128]{2,1,0:T(8,128)(2,1)S(1)}, bf16[128,64,128]{2,1,0:T(8,128)(2,1)}, u32[]{:S(2)}) copy-start(bf16[128,64,128]{2,1,0:T(8,128)(2,1)} %param.9) | copy-start | bytes 6291460
where the time goes:
time: 705 us; the launch traced here: 694 us
  local copies, waits for them, and re-layouts  176 us (25%)
  waiting for transfers between devices  143 us (20%)
  matrix products  135 us (19%)
  other arithmetic  130 us (18%)
  blocking collectives  60.6 us (9%)
  starting transfers between devices  46.2 us (7%)
    reduce_sum x16, other arithmetic, one_group(): distance = jnp.sum(apart * apart, axis=2)  65.9 us
    all_to_all x1, waiting for transfers between devices, in_one_piece(): lax.all_to_all(both, axis, split_axis=split_dim, concat_axis=concat_dim,...  56.8 us
    gather x2, local copies, waits for them, and re-layouts, per_device(): wanted = jnp.take(final_bricks, jnp.maximum(got_ids, 0), axis=0)  53.5 us
    all_to_all x1, waiting for transfers between devices, route_back(): lax.all_to_all(values, ('px', 'py'), split_axis=0, concat_axis=0, tiled=T...  52 us
    dot_general x16, matrix products, one_group(): jnp.einsum('dqw,dewn->deqn', feature_share, kernel_weight_value, preferre...  47.4 us
    dynamic_update_slice x16, other arithmetic, block_work(): kernel_weight_value, brick_tile_grid = lax.map(one_group, grouped)  34.6 us
    unnamed x31, local copies, waits for them, and re-layouts  25.3 us
    dot_general x1, matrix products, decode_points(): jnp.einsum('nhcx,nhpx->ncp', brick_values, kernel_weight_value, preferred...  22.3 us
  transfers between devices with their start and end apart: 6, of which 5 were waited for; matrix products, arithmetic and copies ran while one was open for 3% of the time, Pallas kernels for 0%

commit v1 on v0

v1 whole, which is shorter than its diff:
```python
import functools
import math

import jax
import jax.numpy as jnp
import numpy as np
from jax import lax
from jax.experimental import pallas as pl
from jax.experimental.pallas import tpu as pltpu
from jax.sharding import PartitionSpec as P

CH = 64
MODES = 32
LAYERS = 2
DEV = 128
AMPLITUDE = 0.25
SPREAD = 4.5
DECODE_SCALE = 0.1
BF = jnp.bfloat16
F32 = jnp.float32
MIB = 1024 * 1024
NT = (((1,), (1,)), ((), ()))


def halves(table):
    high = np.asarray(table, np.float32).astype(BF)
    low = (np.asarray(table, np.float64) - high.astype(np.float64)).astype(np.float32).astype(BF)
    return high, low


def waves():
    j = np.arange(MODES)
    return np.where(j < MODES // 2, j, j - MODES)


def turn(frequency, place):
    return 2.0 * math.pi / 128 * ((frequency * place) % 128)


def forward_pair(angle):
    c, s = np.cos(angle) / math.sqrt(128), np.sin(angle) / math.sqrt(128)
    return np.array([[c, s], [-s, c]])


def backward_pair(angle):
    c, s = np.cos(angle) / math.sqrt(128), np.sin(angle) / math.sqrt(128)
    return np.array([[c, -s], [s, c]])


@functools.lru_cache(None)
def tables():
    k = np.arange(MODES)
    z = np.arange(128)
    angle = turn(k[:, None], z[None, :])
    mz = np.stack([np.cos(angle), -np.sin(angle)], 1).reshape(64, 128) / math.sqrt(128)
    mz_high, mz_low = halves(mz)
    z_forward = np.concatenate([mz_high, mz_low], 0)
    weight = np.where(k == 0, 1.0, 2.0)[:, None, None]
    inv = np.stack([np.cos(angle), -np.sin(angle)], 1) / math.sqrt(128) * weight
    inv = inv.reshape(8, 8, 128)
    zi = np.zeros((2, 128, 8, 2, 8))
    for y2 in range(2):
        zi[y2, :, :, y2, :] = inv.transpose(2, 0, 1)
    z_back = np.concatenate(halves(zi.reshape(256, 128)), 1)
    f = waves()
    y = np.arange(128)
    pair = forward_pair(turn(f[:, None], y[None, :])).reshape(2, 2, 16, 2, 32, 4)
    ty = np.zeros((4, 16, 2, 2, 32, 4, 4, 2))
    for k4 in range(4):
        ty[k4, :, :, :, :, :, k4, :] = pair.transpose(2, 3, 0, 4, 5, 1)
    y_forward = np.concatenate(halves(ty.reshape(256, 1024)), 0)
    pair = backward_pair(turn(f[:, None], y[None, :])).reshape(2, 2, 16, 2, 32, 4)
    ti = np.zeros((32, 4, 4, 2, 4, 16, 2, 2))
    for k4 in range(4):
        ti[:, :, k4, :, k4, :, :, :] = pair.transpose(4, 5, 0, 2, 3, 1)
    y_back = np.concatenate(halves(ti.reshape(1024, 256)), 1)
    x = np.arange(128)
    pair = forward_pair(turn(f[:, None], x[None, :])).reshape(2, 2, 32, 16, 4, 2)
    tx = np.zeros((32, 2, 2, 16, 2, 4, 2, 2))
    for ky in range(2):
        tx[:, ky, :, :, :, :, ky, :] = pair.transpose(2, 0, 3, 5, 4, 1)
    x_forward = np.concatenate(halves(tx.reshape(128, 512)), 0)
    pair = backward_pair(turn(f[:, None], x[None, :])).reshape(2, 2, 32, 16, 4, 2)
    txi = np.zeros((16, 2, 4, 2, 2, 2, 32, 2))
    for ky in range(2):
        txi[:, :, :, ky, :, :, :, ky] = pair.transpose(3, 5, 4, 0, 1, 2)
    high, low = halves(txi.reshape(512, 128))
    x_back = np.concatenate([high, low, high], 1)
    order = np.arange(512).reshape(8, 16, 4).transpose(1, 0, 2).reshape(-1)
    to_send = np.eye(512)[order].astype(BF)
    from_send = np.ascontiguousarray(np.eye(512)[order].T).astype(BF)
    row = np.arange(512)
    repeat = np.eye(128)[(row // 8) * 2 + row % 2].astype(BF)
    return dict(
        z_forward=z_forward, z_back=z_back, y_forward=y_forward, y_back=y_back,
        x_forward=x_forward, x_back=x_back, to_send=to_send, from_send=from_send,
        repeat=repeat, eye=np.eye(256).astype(BF),
    )


def dot(a, b):
    return jnp.dot(a, b, preferred_element_type=F32)


def dot_nt(a, b):
    return lax.dot_general(a, b, NT, preferred_element_type=F32)


def call(body, out_shape, *args, scratch=(), specs=None, out_specs=None, limit=40):
    vm = pl.BlockSpec(memory_space=pltpu.VMEM)
    single = not isinstance(out_shape, (tuple, list))
    if specs is None:
        specs = [vm] * len(args)
    if out_specs is None:
        out_specs = vm if single else [vm] * len(out_shape)
    return pl.pallas_call(
        body,
        out_shape=out_shape,
        in_specs=specs,
        out_specs=out_specs,
        scratch_shapes=list(scratch),
        compiler_params=pltpu.CompilerParams(vmem_limit_bytes=limit * MIB),
    )(*args)


VM = pl.BlockSpec(memory_space=pltpu.VMEM)
SM = pl.BlockSpec(memory_space=pltpu.SMEM)


def shaped(shape, dtype=BF):
    return jax.ShapeDtypeStruct(shape, dtype)


def pack_body(bricks, counts, values, offsets, send, slots, seen, aux):
    def clear(d, _):
        send[d] = jnp.zeros((136, 128), BF)
        aux[d] = jnp.zeros((8, 128), F32)
        seen[d] = 0
        return 0

    lax.fori_loop(0, DEV, clear, 0, unroll=4)
    lane = lax.broadcasted_iota(jnp.int32, (1, 128), 1)
    half = lax.broadcasted_iota(jnp.int32, (8, 128), 0) // 4

    def one(b, _):
        first = bricks[4 * b]
        owner = first // 128
        rank = seen[owner]
        seen[owner] = rank + 1
        slots[b] = owner * 2 + rank
        base = owner * 128
        send[owner, pl.ds(pl.multiple_of(rank * 64, 64), 64), :] = values[b]
        meta = jnp.where(lane == 0, counts[b], 0)
        for h in range(4):
            meta = jnp.where(lane == 1 + h, bricks[4 * b + h] - base, meta)
        rows = jnp.concatenate([offsets[b].astype(F32), meta.astype(F32)], 0)
        both = jnp.concatenate([rows, rows], 0)
        aux[owner] = aux[owner] + jnp.where(half == rank, both, 0.0)
        return 0

    lax.fori_loop(0, DEV, one, 0, unroll=2)

    def finish(d, _):
        send[d, 128:136, :] = aux[d].astype(BF)
        return 0

    lax.fori_loop(0, DEV, finish, 0, unroll=4)


def pack(values, offsets, counts, bricks):
    return call(
        pack_body,
        (shaped((DEV, 136, 128)), shaped((DEV,), jnp.int32)),
        bricks.reshape(-1), counts, values, offsets,
        scratch=(pltpu.SMEM((DEV,), jnp.int32), pltpu.VMEM((DEV, 8, 128), F32)),
        specs=[SM, SM, VM, VM],
        out_specs=[VM, SM],
        limit=32,
    )


def anchor(local):
    return (
        (2 * (local // 32)).astype(F32),
        (4 * ((local // 8) % 4)).astype(F32),
        (16 * (local % 8)).astype(F32),
    )


def spread_weights(place, count, ids):
    lane = lax.broadcasted_iota(jnp.int32, (1, 128), 1)
    sub = lax.broadcasted_iota(jnp.int32, (8, 128), 0)
    xs = (sub // 4).astype(F32) + 0.5
    ys = (sub % 4).astype(F32) + 0.5
    zs = lax.broadcasted_iota(jnp.int32, (16, 128), 0).astype(F32) + 0.5
    qx = jnp.where(lane < count, place[0:1], 1.0e4)
    qy = place[1:2]
    qz = place[2:3]
    x0, y0, z0 = anchor(ids[0])
    parts = []
    for h in range(4):
        xh, yh, zh = anchor(ids[h])
        dx = (qx - (xh - x0)) - xs
        dy = (qy - (yh - y0)) - ys
        dz = (qz - (zh - z0)) - zs
        xy = AMPLITUDE * jnp.exp(-(dx * dx + dy * dy) / SPREAD)
        zz = jnp.exp(-(dz * dz) / SPREAD)
        for i in range(8):
            parts.append((xy[i : i + 1] * zz).astype(BF))
    return jnp.concatenate(parts, 0)


def third_forward(grid_at, table, out):
    for by in range(4):
        for j in range(4):
            modes = []
            for half in range(2):
                both = dot(table, grid_at(by, 2 * j + half))
                modes.append(both[:64] + both[64:])
            for kg in range(8):
                piece = jnp.concatenate([m[8 * kg : 8 * kg + 8] for m in modes], 0)
                at = by * 64 + j * 16
                out[kg, at : at + 16, :] = piece.astype(BF)


def encode_body(meta, got, eye, z_table, grid, modes, acc):
    def clear(b, _):
        acc[b] = jnp.zeros((64, 128), F32)
        return 0

    lax.fori_loop(0, 128, clear, 0, unroll=4)

    def one(d, _):
        rows = got[d, 128:136, :].astype(F32)
        for r in range(2):
            at = d * 10 + r * 5
            ids = [meta[at + 1 + h] for h in range(4)]
            weights = spread_weights(rows[4 * r : 4 * r + 3], meta[at], ids)
            tile = dot_nt(got[d, 64 * r : 64 * r + 64, :], weights)
            for h in range(4):
                acc[ids[h]] = acc[ids[h]] + tile[:, 128 * h : 128 * h + 128]
        return 0

    lax.fori_loop(0, DEV, one, 0, unroll=2)
    eye128 = eye[0:128, 0:128]
    for by in range(4):
        for bz in range(8):
            bricks = jnp.concatenate([acc[(bx * 4 + by) * 8 + bz] for bx in range(4)], 0)
            cells = dot_nt(eye128, bricks.astype(BF)).astype(BF)
            for xy in range(8):
                grid[by, xy, 16 * bz : 16 * bz + 16, :] = cells[16 * xy : 16 * xy + 16]
    third_forward(lambda by, xy: grid[by, xy], z_table[...], modes)


def encode(meta, got, t):
    return call(
        encode_body,
        (shaped((4, 8, 128, 256)), shaped((8, 256, 256))),
        meta, got, t["eye"], t["z_forward"],
        scratch=(pltpu.VMEM((128, 64, 128), F32),),
        specs=[SM, VM, VM, VM],
        limit=40,
    )


def second_body(got, table, order, send):
    rows = []
    for x2 in range(2):
        data = jnp.concatenate(
            [
                got[py, by * 64 + x2 * 32 : by * 64 + x2 * 32 + 32, :]
                for py in range(8)
                for by in range(4)
            ],
            0,
        )
        both = dot(table[...], data)
        out = both[:256] + both[256:]
        for bx in range(4):
            rows.append(
                jnp.concatenate(
                    [out[64 * k : 64 * k + 64, 64 * bx : 64 * bx + 64] for k in range(4)], 1
                ).astype(BF)
            )
    send[...] = dot(order[...], jnp.concatenate(rows, 0)).astype(BF)


def mix_body(got, weights, forward, back, repeat, send, product):
    both = dot(forward[...], got[...])
    modes = (both[:128] + both[128:]).astype(BF)
    spread = dot(repeat[...], modes)
    row = lax.broadcasted_iota(jnp.int32, (512, 256), 0)
    col = lax.broadcasted_iota(jnp.int32, (512, 256), 1)
    spread = jnp.where(col // 64 == (row % 8) // 2, spread, 0.0)
    for m in range(64):
        product[8 * m : 8 * m + 8, :] = dot(spread[8 * m : 8 * m + 8].astype(BF), weights[m])
    real, imag = [], []
    for kz in range(4):
        from_real = product[pl.ds(2 * kz, 64, stride=8), :]
        from_imag = product[pl.ds(2 * kz + 1, 64, stride=8), :]
        real.append(from_real[:, :64] - from_imag[:, 64:])
        imag.append(from_real[:, 64:] + from_imag[:, :64])
    mixed = jnp.concatenate([jnp.concatenate(real, 1), jnp.concatenate(imag, 1)], 0)
    high = mixed.astype(BF)
    low = (mixed - high.astype(F32)).astype(BF)
    send[...] = dot(back[...], jnp.concatenate([high, high, low], 0)).astype(BF)


def second_back_body(got, table, order, send):
    ordered = dot(order[...], got[...])
    for x2 in range(2):
        parts = []
        for k in range(4):
            parts.append(
                jnp.concatenate(
                    [
                        ordered[
                            (x2 * 4 + bx) * 64 : (x2 * 4 + bx) * 64 + 64, 64 * k : 64 * k + 64
                        ]
                        for bx in range(4)
                    ],
                    1,
                ).astype(BF)
            )
        data = jnp.concatenate(parts, 0)
        out = dot(table[...], jnp.concatenate([data, data], 0)).astype(BF)
        for py in range(8):
            for by in range(4):
                at = py * 128 + by * 32
                send[py, by * 64 + x2 * 32 : by * 64 + x2 * 32 + 32, :] = out[at : at + 32]


def layer_values(by, j, got, grid, z_back, skip, bias):
    at = by * 64 + j * 16
    data = jnp.concatenate([got[kg, at : at + 16, :] for kg in range(8)], 0)
    total = dot(z_back, jnp.concatenate([data, data], 0))
    total = total + dot(grid[by, 2 * j : 2 * j + 2].reshape(256, 256), skip)
    total = total + bias
    result = 0.5 * total * (1.0 + lax.erf(total * math.sqrt(0.5)))
    return result.astype(BF)


def inner_layer_body(got, grid, z_back, skip, bias, z_table, new_grid, modes):
    for by in range(4):
        for j in range(4):
            values = layer_values(by, j, got, grid, z_back[...], skip[...], bias[...])
            new_grid[by, 2 * j] = values[:128]
            new_grid[by, 2 * j + 1] = values[128:]
    third_forward(lambda by, xy: new_grid[by, xy], z_table[...], modes)


def last_layer_body(got, grid, z_back, skip, bias, eye, bricks):
    for by in range(4):
        values = [
            layer_values(by, j, got, grid, z_back[...], skip[...], bias[...]) for j in range(4)
        ]
        for bz in range(8):
            cells = jnp.concatenate(
                [
                    values[xy // 2][(xy % 2) * 128 + 16 * bz : (xy % 2) * 128 + 16 * bz + 16]
                    for xy in range(8)
                ],
                0,
            )
            turned = dot_nt(eye[...], cells).astype(BF)
            for bx in range(4):
                bricks[(bx * 4 + by) * 8 + bz] = turned[64 * bx : 64 * bx + 64]


def decode_body(meta, got, bricks, reply):
    def one(d, _):
        rows = got[d, 128:136, :].astype(F32)
        for r in range(2):
            at = d * 10 + r * 5
            ids = [meta[at + 1 + h] for h in range(4)]
            weights = spread_weights(rows[4 * r : 4 * r + 3], meta[at], ids)
            near = jnp.concatenate([bricks[ids[h]] for h in range(4)], 1)
            reply[d, 64 * r : 64 * r + 64, :] = (DECODE_SCALE * dot(near, weights)).astype(BF)
        return 0

    lax.fori_loop(0, DEV, one, 0, unroll=2)


def pick_body(slots, got, out):
    def one(b, _):
        out[b] = got[slots[b]]
        return 0

    lax.fori_loop(0, DEV, one, 0, unroll=4)


def exchange(x, axis):
    return lax.all_to_all(x, axis, split_axis=0, concat_axis=0, tiled=True)


def per_device(values, offsets, counts, bricks, spectral_weights, skip_weights, skip_bias):
    t = tables()
    t = {name: jnp.asarray(table) for name, table in t.items()}
    send, slots = pack(values, offsets, counts, bricks)
    got = exchange(send, ("px", "py"))
    meta = got[:, 128:, :5].reshape(DEV, 2, 4, 5)[:, :, 3].astype(jnp.int32).reshape(-1)
    grid, modes = encode(meta, got, t)
    for layer in range(LAYERS):
        columns = exchange(modes, "py")
        second = call(
            second_body, shaped((512, 256)), columns, t["y_forward"], t["to_send"], limit=24
        )
        lines = exchange(second.reshape(16, 32, 256), "px").reshape(512, 256)
        back = call(
            mix_body,
            shaped((512, 256)),
            lines,
            spectral_weights[layer].reshape(64, 256, 128),
            t["x_forward"],
            t["x_back"],
            t["repeat"],
            scratch=(pltpu.VMEM((512, 128), F32),),
            limit=24,
        )
        lines = exchange(back.reshape(16, 32, 256), "px").reshape(512, 256)
        columns = call(
            second_back_body,
            shaped((8, 256, 256)),
            lines,
            t["y_back"],
            t["from_send"],
            limit=24,
        )
        columns = exchange(columns, "py")
        skip = jnp.kron(jnp.eye(4, dtype=BF), skip_weights[layer])
        bias = jnp.tile(skip_bias[layer], 4)[None, :]
        if layer + 1 < LAYERS:
            grid, modes = call(
                inner_layer_body,
                (shaped((4, 8, 128, 256)), shaped((8, 256, 256))),
                columns, grid, t["z_back"], skip, bias, t["z_forward"],
                limit=32,
            )
        else:
            final = call(
                last_layer_body,
                shaped((128, 64, 128)),
                columns, grid, t["z_back"], skip, bias, t["eye"],
                limit=32,
            )
    reply = call(
        decode_body, shaped((DEV, 128, 128)), meta, got, final, specs=[SM, VM, VM], limit=32
    )
    returned = exchange(reply, ("px", "py"))
    return call(
        pick_body,
        shaped((DEV, 64, 128)),
        slots, returned.reshape(2 * DEV, 64, 128),
        specs=[SM, VM],
        limit=32,
    )


def solution(mesh):
    return jax.shard_map(
        per_device,
        mesh=mesh,
        in_specs=(
            P(("px", "py"), None, None),
            P(("px", "py"), None, None),
            P(("px", "py")),
            P(("px", "py"), None),
            P(None, None, "px", "py", None, None),
            P(),
            P(),
        ),
        out_specs=P(("px", "py"), None, None),
        check_vma=False,
    )
```

time: 705 us -> 351 us (0.50); the launches traced: 694 us -> 350 us
  local copies, waits for them, and re-layouts: 176 us -> 32.6 us
  matrix products: 135 us -> 0 us
  blocking collectives: 60.6 us -> 195 us
  other arithmetic: 130 us -> 1.16 us
  waiting for transfers between devices: 143 us -> 24.3 us
  Pallas kernels: 0 us -> 79.2 us
  starting transfers between devices: 46.2 us -> 16.8 us
    dot_general x34 -> x0, matrix products: 135 us -> none  [the longest x16 47.4 us: one_group(): jnp.einsum('dqw,dewn->deqn', feature_share, kernel_weight_value, preferre...]
    all_to_all x5 -> x7, blocking collectives: 60.6 us -> 195 us  [exchange(): return lax.all_to_all(x, axis, split_axis=0, concat_axis=0, tiled=True)]
    all_to_all x6 -> x3, waiting for transfers between devices: 143 us -> 24.3 us  [exchange(): return lax.all_to_all(x, axis, split_axis=0, concat_axis=0, tiled=True)]
    pallas_call x0 -> x12, Pallas kernels: none -> 79.2 us  [call(): pl.pallas_call(body, out_shape=out_shape, in_specs=specs, out_specs=out_s...]
    reduce_sum x18 -> x0, other arithmetic: 66.2 us -> none  [the longest x16 65.9 us: one_group(): distance = jnp.sum(apart * apart, axis=2)]
    gather x8 -> x0, local copies, waits for them, and re-layouts: 65 us -> none  [the longest x2 53.5 us: per_device(): wanted = jnp.take(final_bricks, jnp.maximum(got_ids, 0), axis=0)]
    dynamic_update_slice x16 -> x0, other arithmetic: 34.6 us -> none  [block_work(): kernel_weight_value, brick_tile_grid = lax.map(one_group, grouped)]
    convert_element_type x12 -> x1, local copies, waits for them, and re-layouts: 33 us -> 0.22 us  [per_device(): got[:, 128:, :5].reshape(DEV, 2, 4, 5)[:, :, 3].astype(jnp.int32)]
  transfers between devices with their start and end apart: 6 -> 3, of which waited for: 5 -> 2; matrix products, arithmetic and copies ran while one was open for 3% -> 4% of each run, Pallas kernels for 0% -> 0%
where the time goes in v1:
time: 351 us; the launch traced here: 350 us
  blocking collectives  195 us (56%)
  Pallas kernels  79.2 us (23%)
  local copies, waits for them, and re-layouts  32.6 us (9%)
  waiting for transfers between devices  24.3 us (7%)
  starting transfers between devices  16.8 us (5%)
    all_to_all x7, blocking collectives, exchange(): return lax.all_to_all(x, axis, split_axis=0, concat_axis=0, tiled=True)  195 us
    pallas_call x12, Pallas kernels, call(): pl.pallas_call(body, out_shape=out_shape, in_specs=specs, out_specs=out_s...  79.2 us
    all_to_all x3, waiting for transfers between devices, exchange(): return lax.all_to_all(x, axis, split_axis=0, concat_axis=0, tiled=True)  24.3 us
    unnamed x66, local copies, waits for them, and re-layouts  19.5 us
    all_to_all x3, starting transfers between devices, exchange(): return lax.all_to_all(x, axis, split_axis=0, concat_axis=0, tiled=True)  16.8 us
    slice x1, local copies, waits for them, and re-layouts, per_device(): spectral_weights[layer].reshape(64, 256, 128)  7.96 us
  transfers between devices with their start and end apart: 3, of which 2 were waited for; matrix products, arithmetic and copies ran while one was open for 4% of the time, Pallas kernels for 0%

profile of v1, /device:TPU:1, one launch (start us, length us, event | category | flops | bytes accessed | tf_op | source)
XLA Modules:
  0.0 349.6 jit_solution(151699391258516383)
XLA Ops:
  1.9 1.6 copy-done.11
  4.1 4.0 %shard_map.163 = (bf16[128,136,128]{2,1,0:T(8,128)(2,1)S(1)}, s32[128]{0:T(128)S(1)}) custom-call(s32[512]{0:T(512)S(1)} %reshape.58.bricks, s32[128]{0:T(128)S(1)} %copy-done.28, bf16[128,64,128]{2,1,0:T(8,128)(2,1)S(1)} %copy-done.11, bf16[128,3,128]{2,1,0:T(4,128)(2,1)S(1)} %copy.20.offsets), custom_call_target="tpu_custom_call" | custom-call | tf_op jit(solution)/shard_map/pallas_call | solution.py:116
  8.2 67.3 %all_to_all.50.got = bf16[128,136,128]{2,1,0:T(8,128)(2,1)S(1)} all-to-all(bf16[128,136,128]{2,1,0:T(8,128)(2,1)S(1)} %get-tuple-element.12), channel_id=1, replica_groups=mesh['px'=16,'py'=8] {'px','py'}, dimensions={0} | all-to-all | bytes 8912896 | tf_op jit(solution)/shard_map/all_to_all | solution.py:393
  75.5 2.1 copy-done
  78.1 2.3 copy-done.1
  80.3 30.6 %shard_map.164 = (bf16[4,8,128,256]{3,2,1,0:T(8,128)(2,1)S(1)}, bf16[8,256,256]{2,1,0:T(8,128)(2,1)S(1)}) custom-call(s32[1280]{0:T(1024)S(1)} %reshape.69.meta, bf16[128,136,128]{2,1,0:T(8,128)(2,1)S(1)} %copy-done.1, bf16[256,256]{1,0:T(8,128)(2,1)S(1)} %copy-done.19, bf16[128,128]{1,0:T(8,128)(2,1)S(1)} %copy-done.26), custom_call_target="tpu_custom_call" | custom-call | tf_op jit(solution)/shard_map/pallas_call | solution.py:116
  111.0 18.1 %all_to_all.51.got = bf16[8,256,256]{2,1,0:T(8,128)(2,1)S(1)} all-to-all(bf16[8,256,256]{2,1,0:T(8,128)(2,1)S(1)} %get-tuple-element.13), channel_id=1, replica_groups=mesh['px'=16,'py'=8] {'py'}, dimensions={0} | all-to-all | bytes 2097152 | tf_op jit(solution)/shard_map/all_to_all | solution.py:393
  129.1 1.9 shard_map.165
  131.0 3.5 %all-to-all-start.2 = ((bf16[16,32,256]{2,1,0:T(8,128)(2,1)}), bf16[16,32,256]{2,1,0:T(8,128)(2,1)S(1)}, u32[]{:S(2)}, u32[]{:S(2)}) async-start(bf16[16,32,256]{2,1,0:T(8,128)(2,1)} %bitcast.1), calls=%async_computation.2 | async-start | bytes 524288 | tf_op jit(solution)/shard_map/all_to_all | solution.py:393
  134.5 8.0 %fusion.1 = (bf16[1,32,2,4,64,128]{5,4,3,2,1,0:T(8,128)(2,1)}, bf16[1,32,2,4,64,128]{5,4,3,2,1,0:T(8,128)(2,1)}) fusion(bf16[2,32,2,4,64,128]{5,4,3,2,1,0:T(8,128)(2,1)} %param.21), kind=kLoop, calls=%fused_computation.9 | loop fusion | bytes 16777216 | tf_op jit(solution)/shard_map/slice | solution.py:413
  142.5 2.2 copy-done.4
  145.6 1.6 shard_map.166
  147.3 14.0 %all_to_all.52 = bf16[16,32,256]{2,1,0:T(8,128)(2,1)S(1)} all-to-all(bf16[16,32,256]{2,1,0:T(8,128)(2,1)S(1)} %bitcast.31), channel_id=1, replica_groups=mesh['px'=16,'py'=8] {'px'}, dimensions={0} | all-to-all | bytes 524288 | tf_op jit(solution)/shard_map/all_to_all | solution.py:393
  161.2 2.0 shard_map.167
  163.3 6.2 %all-to-all-start.4 = ((bf16[8,256,256]{2,1,0:T(8,128)(2,1)}), bf16[8,256,256]{2,1,0:T(8,128)(2,1)S(1)}, u32[]{:S(2)}, u32[]{:S(2)}) async-start(bf16[8,256,256]{2,1,0:T(8,128)(2,1)} %shard_map.167), calls=%async_computation.4 | async-start | bytes 2097152 | tf_op jit(solution)/shard_map/all_to_all | solution.py:393
  171.3 1.8 mul.49.skip
  174.9 9.6 %all-to-all-done.4.got = bf16[8,256,256]{2,1,0:T(8,128)(2,1)S(1)} async-done(((bf16[8,256,256]{2,1,0:T(8,128)(2,1)}), bf16[8,256,256]{2,1,0:T(8,128)(2,1)S(1)}, u32[]{:S(2)}, u32[]{:S(2)}) %all-to-all-start.4) | async-done | bytes 1048608 | tf_op jit(solution)/shard_map/all_to_all | solution.py:393
  184.5 1.6 copy-done.10
  188.6 1.9 shard_map.168
  190.5 18.3 %all_to_all.53.got = bf16[8,256,256]{2,1,0:T(8,128)(2,1)S(1)} all-to-all(bf16[8,256,256]{2,1,0:T(8,128)(2,1)S(1)} %get-tuple-element.15), channel_id=1, replica_groups=mesh['px'=16,'py'=8] {'py'}, dimensions={0} | all-to-all | bytes 2097152 | tf_op jit(solution)/shard_map/all_to_all | solution.py:393
  210.0 10.3 %all_to_all.54 = bf16[16,32,256]{2,1,0:T(8,128)(2,1)S(1)} all-to-all(bf16[16,32,256]{2,1,0:T(8,128)(2,1)S(1)} %bitcast.25), channel_id=1, replica_groups=mesh['px'=16,'py'=8] {'px'}, dimensions={0} | all-to-all | bytes 524288 | tf_op jit(solution)/shard_map/all_to_all | solution.py:393
  220.3 1.6 shard_map.170
  222.0 10.5 %all_to_all.55 = bf16[16,32,256]{2,1,0:T(8,128)(2,1)S(1)} all-to-all(bf16[16,32,256]{2,1,0:T(8,128)(2,1)S(1)} %bitcast.30), channel_id=1, replica_groups=mesh['px'=16,'py'=8] {'px'}, dimensions={0} | all-to-all | bytes 524288 | tf_op jit(solution)/shard_map/all_to_all | solution.py:393
  232.5 2.1 shard_map.171
  234.6 7.1 %all-to-all-start.8 = ((bf16[8,256,256]{2,1,0:T(8,128)(2,1)}), bf16[8,256,256]{2,1,0:T(8,128)(2,1)S(1)}, u32[]{:S(2)}, u32[]{:S(2)}) async-start(bf16[8,256,256]{2,1,0:T(8,128)(2,1)} %shard_map.171), calls=%async_computation.8 | async-start | bytes 2097152 | tf_op jit(solution)/shard_map/all_to_all | solution.py:393
  242.0 14.7 %all-to-all-done.8.got = bf16[8,256,256]{2,1,0:T(8,128)(2,1)S(1)} async-done(((bf16[8,256,256]{2,1,0:T(8,128)(2,1)}), bf16[8,256,256]{2,1,0:T(8,128)(2,1)S(1)}, u32[]{:S(2)}, u32[]{:S(2)}) %all-to-all-start.8) | async-done | bytes 1048608 | tf_op jit(solution)/shard_map/all_to_all | solution.py:393
  256.7 1.6 copy-done.8
  258.3 3.0 shard_map.172.bricks
  261.2 2.3 copy-done.2
  263.5 27.0 %shard_map.173 = bf16[128,128,128]{2,1,0:T(8,128)(2,1)S(1)} custom-call(s32[1280]{0:T(1024)S(1)} %reshape.69.meta, bf16[128,136,128]{2,1,0:T(8,128)(2,1)S(1)} %copy-done.2, bf16[128,64,128]{2,1,0:T(8,128)(2,1)S(1)} %shard_map.172.bricks), custom_call_target="tpu_custom_call" | custom-call | tf_op jit(solution)/shard_map/pallas_call | solution.py:116
  290.5 56.9 %all_to_all.56 = bf16[128,128,128]{2,1,0:T(8,128)(2,1)S(1)} all-to-all(bf16[128,128,128]{2,1,0:T(8,128)(2,1)S(1)} %shard_map.173), channel_id=1, replica_groups=mesh['px'=16,'py'=8] {'px','py'}, dimensions={0} | all-to-all | bytes 8388608 | tf_op jit(solution)/shard_map/all_to_all | solution.py:393
  347.4 2.2 shard_map.174
  (75 shorter events, 11.6 us)
Async XLA Ops:
  1.9 1.6 copy-start.11
  8.2 69.9 %copy-start.19 = (bf16[256,256]{1,0:T(8,128)(2,1)S(1)}, bf16[256,256]{1,0:T(8,128)(2,1)}, u32[]{:S(2)}) copy-start(bf16[256,256]{1,0:T(8,128)(2,1)} %constant.29.clone.eye) | copy-start | bytes 393220
  8.2 69.9 %copy-start.26 = (bf16[128,128]{1,0:T(8,128)(2,1)S(1)}, bf16[128,128]{1,0:T(8,128)(2,1)}, u32[]{:S(2)}) copy-start(bf16[128,128]{1,0:T(8,128)(2,1)} %constant.20.clone.z_table) | copy-start | bytes 98308
  8.2 120.9 %copy-start.14 = (bf16[512,512]{1,0:T(8,128)(2,1)S(1)}, bf16[512,512]{1,0:T(8,128)(2,1)}, u32[]{:S(2)}) copy-start(bf16[512,512]{1,0:T(8,128)(2,1)} %constant.26.clone.order) | copy-start | bytes 1572868
  75.5 53.6 %copy-start.6 = (bf16[512,1024]{1,0:T(8,128)(2,1)S(1)}, bf16[512,1024]{1,0:T(8,128)(2,1)}, u32[]{:S(2)}) copy-start(bf16[512,1024]{1,0:T(8,128)(2,1)} %constant.22.clone.table) | copy-start | bytes 3145732
  75.5 2.1 copy-start
  78.1 2.3 copy-start.1
  111.0 20.0 %copy-start.9 = (bf16[4,8,128,256]{3,2,1,0:T(8,128)(2,1)}, bf16[4,8,128,256]{3,2,1,0:T(8,128)(2,1)S(1)}, u32[]{:S(2)}) copy-start(bf16[4,8,128,256]{3,2,1,0:T(8,128)(2,1)S(1)} %get-tuple-element.14.grid) | copy-start | bytes 6291460
  131.0 11.5 %all-to-all-start.2 = ((bf16[16,32,256]{2,1,0:T(8,128)(2,1)}), bf16[16,32,256]{2,1,0:T(8,128)(2,1)S(1)}, u32[]{:S(2)}, u32[]{:S(2)}) async-start(bf16[16,32,256]{2,1,0:T(8,128)(2,1)} %bitcast.1), calls=%async_computation.2 | async-start | bytes 524288 | tf_op jit(solution)/shard_map/all_to_all | solution.py:393
  134.5 8.0 %copy-start.16 = (bf16[512,384]{1,0:T(8,128)(2,1)S(1)}, bf16[512,384]{1,0:T(8,128)(2,1)}, u32[]{:S(2)}) copy-start(bf16[512,384]{1,0:T(8,128)(2,1)} %constant.25.clone.back) | copy-start | bytes 1179652
  134.5 8.0 %copy-start.17 = (bf16[256,512]{1,0:T(8,128)(2,1)S(1)}, bf16[256,512]{1,0:T(8,128)(2,1)}, u32[]{:S(2)}) copy-start(bf16[256,512]{1,0:T(8,128)(2,1)} %constant.24.clone.forward) | copy-start | bytes 786436
  134.5 26.7 %copy-start.5 = (bf16[1024,512]{1,0:T(8,128)(2,1)S(1)}, bf16[1024,512]{1,0:T(8,128)(2,1)}, u32[]{:S(2)}) copy-start(bf16[1024,512]{1,0:T(8,128)(2,1)} %constant.23.clone.table) | copy-start | bytes 3145732
  134.5 26.7 %copy-start.12 = (bf16[512,512]{1,0:T(8,128)(2,1)S(1)}, bf16[512,512]{1,0:T(8,128)(2,1)}, u32[]{:S(2)}) copy-start(bf16[512,512]{1,0:T(8,128)(2,1)} %constant.27.clone.order) | copy-start | bytes 1572868
  142.5 2.2 copy-start.4
  144.7 0.9 copy-start.23
  147.2 25.9 %copy-start.31 = (f32[2,64]{1,0:T(2,128)S(1)}, f32[2,64]{1,0:T(2,128)}, u32[]{:S(2)}) copy-start(f32[2,64]{1,0:T(2,128)} %param.23) | copy-start | bytes 1540
  163.3 21.2 %all-to-all-start.4 = ((bf16[8,256,256]{2,1,0:T(8,128)(2,1)}), bf16[8,256,256]{2,1,0:T(8,128)(2,1)S(1)}, u32[]{:S(2)}, u32[]{:S(2)}) async-start(bf16[8,256,256]{2,1,0:T(8,128)(2,1)} %shard_map.167), calls=%async_computation.4 | async-start | bytes 2097152 | tf_op jit(solution)/shard_map/all_to_all | solution.py:393
  184.5 1.6 copy-start.10
  186.1 0.9 copy-start.21
  188.6 20.2 %copy-start.15 = (bf16[512,512]{1,0:T(8,128)(2,1)S(1)}, bf16[512,512]{1,0:T(8,128)(2,1)}, u32[]{:S(2)}) copy-start(bf16[512,512]{1,0:T(8,128)(2,1)} %constant.26.clone.order) | copy-start | bytes 1572868
  188.6 31.7 %copy-start.3 = (bf16[1,32,2,4,64,128]{5,4,3,2,1,0:T(8,128)(2,1)S(1)}, bf16[1,32,2,4,64,128]{5,4,3,2,1,0:T(8,128)(2,1)}, u32[]{:S(2)}) copy-start(bf16[1,32,2,4,64,128]{5,4,3,2,1,0:T(8,128)(2,1)} %get-tuple-element.17) | copy-start | bytes 12582916
  188.6 31.7 %copy-start.18 = (bf16[256,512]{1,0:T(8,128)(2,1)S(1)}, bf16[256,512]{1,0:T(8,128)(2,1)}, u32[]{:S(2)}) copy-start(bf16[256,512]{1,0:T(8,128)(2,1)} %constant.24.clone.forward) | copy-start | bytes 786436
  188.6 31.7 %copy-start.24 = (bf16[512,128]{1,0:T(8,128)(2,1)S(1)}, bf16[512,128]{1,0:T(8,128)(2,1)}, u32[]{:S(2)}) copy-start(bf16[512,128]{1,0:T(8,128)(2,1)} %constant.28.clone.repeat) | copy-start | bytes 393220
  190.5 31.5 %copy-start.7 = (bf16[4,8,128,256]{3,2,1,0:T(8,128)(2,1)}, bf16[4,8,128,256]{3,2,1,0:T(8,128)(2,1)S(1)}, u32[]{:S(2)}) copy-start(bf16[4,8,128,256]{3,2,1,0:T(8,128)(2,1)S(1)} %get-tuple-element.16.grid) | copy-start | bytes 6291460
  208.8 23.7 %copy-start.13 = (bf16[512,512]{1,0:T(8,128)(2,1)S(1)}, bf16[512,512]{1,0:T(8,128)(2,1)}, u32[]{:S(2)}) copy-start(bf16[512,512]{1,0:T(8,128)(2,1)} %constant.27.clone.order) | copy-start | bytes 1572868
  220.3 21.3 %copy-start.29 = (bf16[4,64,4,64]{3,2,1,0:T(4,128)(2,1)S(1)}, bf16[4,64,4,64]{3,2,1,0:T(4,128)(2,1)}, u32[]{:S(2)}) copy-start(bf16[4,64,4,64]{3,2,1,0:T(4,128)(2,1)} %get-tuple-element.23) | copy-start | bytes 393220
  222.0 19.9 %copy-start.30 = (f32[64]{0:T(128)S(1)}, f32[64]{0:T(128)}, u32[]{:S(2)}) copy-start(f32[64]{0:T(128)} %get-tuple-element.21) | copy-start | bytes 772
  222.0 34.7 %copy-start.20 = (bf16[256,256]{1,0:T(8,128)(2,1)S(1)}, bf16[256,256]{1,0:T(8,128)(2,1)}, u32[]{:S(2)}) copy-start(bf16[256,256]{1,0:T(8,128)(2,1)} %constant.29.clone.eye) | copy-start | bytes 393220
  222.0 34.6 %copy-start.22 = (bf16[256,256]{1,0:T(8,128)(2,1)S(1)}, bf16[256,256]{1,0:T(8,128)(2,1)}, u32[]{:S(2)}) copy-start(bf16[256,256]{1,0:T(8,128)(2,1)} %constant.21.clone.z_back) | copy-start | bytes 393220
  234.6 22.1 %all-to-all-start.8 = ((bf16[8,256,256]{2,1,0:T(8,128)(2,1)}), bf16[8,256,256]{2,1,0:T(8,128)(2,1)S(1)}, u32[]{:S(2)}, u32[]{:S(2)}) async-start(bf16[8,256,256]{2,1,0:T(8,128)(2,1)} %shard_map.171), calls=%async_computation.8 | async-start | bytes 2097152 | tf_op jit(solution)/shard_map/all_to_all | solution.py:393
  256.7 1.6 copy-start.8
  261.2 2.3 copy-start.2
  (3 other events, 2.3 us)
